TPU v7x, 32 devices: a whole 2x2x4 slice. The times are simulated.
32 devices in a mesh: gx: 4 (over z), wa: 8 (over y, x, core).
Axes of the slice: x: 2, y: 2, z: 4, core: 2. Of those that a mesh axis runs over, the one named last changes fastest.
Arguments:
- positions: float32 [512, 3, 256], P(('gx', 'wa')), may hold values from 0 to 1
- weights: float32 [512, 256], P(('gx', 'wa')), may hold values from 0.5 to 2
- block_count: int32 [512], P(('gx', 'wa')), may hold values from 1 to 256
- send_list: int32 [32, 8, 2], P(('gx', 'wa')), may hold values from 0 to 15
- unit_pair: int32 [32, 16], P(('gx', 'wa')), may hold values from 0 to 15, each once within a row
- unit_live: int32 [32], P(('gx', 'wa')), may hold values from 2 to 16, as said below
Outputs:
- slab_counts: float32 [4, 30, 20], P('gx')
- totals: float32 [30, 20], replicated
Inputs may be any that keep to these rules, and one draw needn't show every extreme that they name: `unit_pair`: each row holds every slot number once. `unit_live`: the active units of a device are the first ones of its list; some device has all 16 active.
All inputs are finite; a program needn't handle non-finite values.
Results may differ from a plain program's by a relative error of at most 0.0003.
Values sent between devices are 32-bit elements; how exact they have to be, the bound alone decides.
No kernel may reach another device: no remote copies, remote signals or barrier semaphores. Data moves between devices by JAX's collectives and lax.ppermute only.
A program may use at most 64 MiB of HBM per device.

v0:
```python
import jax
import jax.numpy as jnp
from jax import lax
from jax.sharding import PartitionSpec as P

SBINS = 30
MUBINS = 20
reach = 0.5
viewer = (0.5, 0.5, -1.5)
units_per_turn = 4


def passed_along(shard, axis, by):
    count = lax.axis_size(axis)
    return lax.ppermute(shard, axis, [(i, (i + by) % count) for i in range(count)])


def group_counts(a_pos, a_wgt, b_pos, b_wgt):
    step = reach / SBINS
    diff = a_pos[:, :, :, None] - b_pos[:, :, None, :]
    eye_at = jnp.array(viewer, dtype=jnp.float32)[None, :, None, None]
    middle = 0.5 * (a_pos[:, :, :, None] + b_pos[:, :, None, :]) + eye_at
    square = jnp.sum(diff * diff, axis=1)
    dist = jnp.sqrt(square)
    along = jnp.abs(jnp.sum(diff * middle, axis=1)) / jnp.sqrt(
        jnp.maximum(square, step * step) * jnp.sum(middle * middle, axis=1)
    )
    s_mid = jnp.arange(SBINS, dtype=jnp.float32) + 0.5
    m_mid = jnp.arange(MUBINS, dtype=jnp.float32) + 0.5
    s_hat = jnp.maximum(
        0.0, 1.0 - jnp.abs(dist[:, None] / step - s_mid[None, :, None, None])
    ).astype(jnp.bfloat16)
    pair_w = a_wgt[:, :, None] * b_wgt[:, None, :]
    m_hat = (
        jnp.maximum(0.0, 1.0 - jnp.abs(along[:, None] * MUBINS - m_mid[None, :, None, None]))
        * pair_w[:, None]
    ).astype(jnp.bfloat16)
    return jnp.einsum("gkab,gjab->kj", s_hat, m_hat, preferred_element_type=jnp.float32)


def per_device(positions, weights, block_count, send_list, unit_pair, unit_live):
    block = positions.shape[2]
    per_peer = send_list.shape[2]
    peers = lax.axis_size("wa")
    units = peers * per_peer
    live = jnp.arange(block, dtype=jnp.int32)[None, :] < block_count[:, None]
    masked = jnp.where(live, weights, jnp.float32(0.0))
    picks = send_list[0].reshape(-1)
    send_pos = positions[picks].reshape(peers, per_peer, 3, block)
    send_wgt = masked[picks].reshape(peers, per_peer, block)
    own_pos, own_wgt = (
        lax.all_to_all(send_pos, "wa", split_axis=0, concat_axis=0, tiled=True),
        lax.all_to_all(send_wgt, "wa", split_axis=0, concat_axis=0, tiled=True),
    )
    below_pos, below_wgt = passed_along((own_pos, own_wgt), "gx", 1)
    own_pos = own_pos.reshape(units, 3, block)
    own_wgt = own_wgt.reshape(units, block)
    below_pos = below_pos.reshape(units, 3, block)
    below_wgt = below_wgt.reshape(units, block)
    partner = unit_pair[0]
    partner_pos = below_pos[partner]
    partner_wgt = below_wgt[partner]
    active = jnp.arange(units, dtype=jnp.int32) < unit_live[0]
    own_wgt = jnp.where(active[:, None], own_wgt, jnp.float32(0.0))
    start = jnp.zeros((SBINS, MUBINS), jnp.float32)
    turns = units // units_per_turn
    items = (
        own_pos.reshape(turns, units_per_turn, 3, block),
        own_wgt.reshape(turns, units_per_turn, block),
        partner_pos.reshape(turns, units_per_turn, 3, block),
        partner_wgt.reshape(turns, units_per_turn, block),
    )

    def accumulate(total, group):
        return (total + group_counts(*group), None)

    total, _ = lax.scan(accumulate, start, items)
    scale = 10.0 * SBINS * MUBINS / (peers * units * block * block)
    slab = lax.psum(total, "wa") * scale
    whole = lax.psum(slab, "gx") / lax.axis_size("gx")
    return (slab[None], whole)


def solution(mesh):
    return jax.shard_map(
        per_device,
        mesh=mesh,
        in_specs=(
            P(("gx", "wa"), None, None),
            P(("gx", "wa"), None),
            P(("gx", "wa")),
            P(("gx", "wa"), None, None),
            P(("gx", "wa"), None),
            P(("gx", "wa")),
        ),
        out_specs=(P("gx", None, None), P()),
        check_vma=False,
    )
```

profile of v0, /device:TPU:0, one launch (start us, length us, event | category | flops | bytes accessed | tf_op | source)
XLA Modules:
  0.0 132.2 jit_solution(15789836194075726807)
XLA Ops:
  0.7 0.8 copy.30
  1.5 0.8 fusion.12
  2.3 0.6 gather_fusion.2
  2.9 0.6 reshape.132
  3.5 5.2 %all-to-all-start.1 = ((f32[8,2,256]{2,1,0:T(2,128)}), f32[8,2,256]{2,1,0:T(2,128)S(1)}, u32[]{:S(2)}, u32[]{:S(2)}) async-start(f32[8,2,256]{2,1,0:T(2,128)} %reshape.132), calls=%async_computation.1 | async-start | bytes 32768 | tf_op jit(solution)/shard_map/all_to_all | solution.py:53
  8.7 0.7 fusion.14
  9.4 0.6 gather_fusion
  10.0 0.6 copy.31
  11.3 2.1 %all-to-all-done.1 = f32[8,2,256]{2,1,0:T(2,128)S(1)} async-done(((f32[8,2,256]{2,1,0:T(2,128)}), f32[8,2,256]{2,1,0:T(2,128)S(1)}, u32[]{:S(2)}, u32[]{:S(2)}) %all-to-all-start.1) | async-done | bytes 16416 | tf_op jit(solution)/shard_map/all_to_all | solution.py:53
  13.5 3.3 %all-to-all-start = ((f32[8,2,3,256]{3,1,2,0:T(2,128)}), f32[8,2,3,256]{3,1,2,0:T(2,128)S(1)}, u32[]{:S(2)}, u32[]{:S(2)}) async-start(f32[8,2,3,256]{3,1,2,0:T(2,128)} %copy.31), calls=%async_computation | async-start | bytes 98304 | tf_op jit(solution)/shard_map/all_to_all | solution.py:52
  16.8 1.6 %collective-permute-start.1 = (f32[8,2,256]{2,1,0:T(2,128)S(1)}, f32[8,2,256]{2,1,0:T(2,128)S(1)}, u32[]{:S(2)}, u32[]{:S(2)}) collective-permute-start(f32[8,2,256]{2,1,0:T(2,128)S(1)} %all-to-all-done.1), channel_id=1, source_target_pairs={{0,8},{8,16},{16,24},{24,0},{1,9},{9,17},{17,25},{25,1},{2,10},{10... | collective-permute-start | bytes 49160 | tf_op jit(solution)/shard_map/ppermute | solution.py:15
  18.5 3.2 %all-to-all-done = f32[8,2,3,256]{3,1,2,0:T(2,128)S(1)} async-done(((f32[8,2,3,256]{3,1,2,0:T(2,128)}), f32[8,2,3,256]{3,1,2,0:T(2,128)S(1)}, u32[]{:S(2)}, u32[]{:S(2)}) %all-to-all-start) | async-done | bytes 49184 | tf_op jit(solution)/shard_map/all_to_all | solution.py:52
  21.7 1.6 %collective-permute-start = (f32[8,2,3,256]{3,1,2,0:T(2,128)S(1)}, f32[8,2,3,256]{3,1,2,0:T(2,128)S(1)}, u32[]{:S(2)}, u32[]{:S(2)}) collective-permute-start(f32[8,2,3,256]{3,1,2,0:T(2,128)S(1)} %all-to-all-done), channel_id=1, source_target_pairs={{0,8},{8,16},{16,24},{24,0},{1,9},{9,17},{17,25},{25,1},{2,10},{10... | collective-permute-start | bytes 147464 | tf_op jit(solution)/shard_map/ppermute | solution.py:15
  23.4 0.6 gather_fusion.3
  24.0 3.6 %collective-permute-done = f32[8,2,3,256]{3,1,2,0:T(2,128)S(1)} collective-permute-done((f32[8,2,3,256]{3,1,2,0:T(2,128)S(1)}, f32[8,2,3,256]{3,1,2,0:T(2,128)S(1)}, u32[]{:S(2)}, u32[]{:S(2)}) %collective-permute-start) | collective-permute-done | bytes 49184 | tf_op jit(solution)/shard_map/ppermute | solution.py:15
  27.6 0.6 gather_fusion.1
  28.2 63.3 %while.12 = (s32[]{:T(128)}, f32[30,20]{0,1:T(8,128)S(1)}, f32[4,4,3,256]{3,2,1,0:T(4,128)S(1)}, f32[4,4,3,256]{3,2,1,0:T(4,128)S(1)}, f32[4,4,256]{2,1,0:T(4,12...) while((s32[]{:T(128)}, f32[30,20]{0,1:T(8,128)S(1)}, ...), condition=%wide.region_4.5_spmd.clone.clone, body=%wide.region_0.4_spmd.sunk.clone.clone.sunk | while | flops 394265856 | bytes 16889040 | solution.py:77
  28.2 1.4 %fusion.17 = (f32[4,256,256]{2,1,0:T(8,128)S(1)}, f32[4,256,256]{2,1,0:T(8,128)S(1)}, f32[4,256,256]{2,1,0:T(8,128)S(1)}) fusion(f32[3]{0:T(128)S(1)} %get-tuple-element.207, f32[4,3,256]{2,1,0:T(4,128)S(1)} %get-tuple-element.175, f32[4,3,256]{2,1,0:T(4,128)S(1)} %get-tuple-element.176), kind=kLoop, calls=%fused_computation.15.clone.1 | loop fusion | flops 7077888 | bytes 3170316 | tf_op jit(solution)/shard_map/while/body/eval_jaxpr/reduce_sum | solution.py:25
  29.7 0.5 sqrt_multiply_fusion.2
  30.2 0.7 copy.44
  30.8 0.7 copy.45
  31.5 0.1 copy.43
  31.7 0.3 broadcast_multiply_fusion.4
  32.1 11.9 %fusion.18 = f32[30,20]{0,1:T(8,128)S(1)} fusion(f32[4,256,256]{2,0,1:T(4,128)S(1)} %broadcast_multiply_fusion.4, f32[20]{0:T(128)S(1)} %iota_add_fusion.4, f32[4,256,256]{2,0,1:T(4,128)S(1)} %copy.44, f32[30]{0:T(128)S(1)} %iota_add_fusion.5, f32[4,256,256]{2,0,1:T(4,128)S(1)} %copy.45, f32[30,20]{0,1:T(8,128)S(1)} %get-tuple-element.192, ...), kind=kOutput, calls=%fused_computation.19.clone.1 | convolution fusion | flops 385352896 | bytes 3150729 | tf_op jit(solution)/shard_map/while/body/eval_jaxpr/gkab,gjab->kj/dot_general | solution.py:38
  44.1 1.4 %fusion.17 = (f32[4,256,256]{2,1,0:T(8,128)S(1)}, f32[4,256,256]{2,1,0:T(8,128)S(1)}, f32[4,256,256]{2,1,0:T(8,128)S(1)}) fusion(f32[3]{0:T(128)S(1)} %get-tuple-element.207, f32[4,3,256]{2,1,0:T(4,128)S(1)} %get-tuple-element.175, f32[4,3,256]{2,1,0:T(4,128)S(1)} %get-tuple-element.176), kind=kLoop, calls=%fused_computation.15.clone.1 | loop fusion | flops 7077888 | bytes 3170316 | tf_op jit(solution)/shard_map/while/body/eval_jaxpr/reduce_sum | solution.py:25
  45.5 0.5 sqrt_multiply_fusion.2
  46.0 0.7 copy.44
  46.7 0.7 copy.45
  47.4 0.1 copy.43
  47.5 0.3 broadcast_multiply_fusion.4
  47.9 11.9 %fusion.18 = f32[30,20]{0,1:T(8,128)S(1)} fusion(f32[4,256,256]{2,0,1:T(4,128)S(1)} %broadcast_multiply_fusion.4, f32[20]{0:T(128)S(1)} %iota_add_fusion.4, f32[4,256,256]{2,0,1:T(4,128)S(1)} %copy.44, f32[30]{0:T(128)S(1)} %iota_add_fusion.5, f32[4,256,256]{2,0,1:T(4,128)S(1)} %copy.45, f32[30,20]{0,1:T(8,128)S(1)} %get-tuple-element.192, ...), kind=kOutput, calls=%fused_computation.19.clone.1 | convolution fusion | flops 385352896 | bytes 3150729 | tf_op jit(solution)/shard_map/while/body/eval_jaxpr/gkab,gjab->kj/dot_general | solution.py:38
  59.9 1.4 %fusion.17 = (f32[4,256,256]{2,1,0:T(8,128)S(1)}, f32[4,256,256]{2,1,0:T(8,128)S(1)}, f32[4,256,256]{2,1,0:T(8,128)S(1)}) fusion(f32[3]{0:T(128)S(1)} %get-tuple-element.207, f32[4,3,256]{2,1,0:T(4,128)S(1)} %get-tuple-element.175, f32[4,3,256]{2,1,0:T(4,128)S(1)} %get-tuple-element.176), kind=kLoop, calls=%fused_computation.15.clone.1 | loop fusion | flops 7077888 | bytes 3170316 | tf_op jit(solution)/shard_map/while/body/eval_jaxpr/reduce_sum | solution.py:25
  61.3 0.5 sqrt_multiply_fusion.2
  61.8 0.7 copy.44
  62.5 0.7 copy.45
  63.3 0.3 broadcast_multiply_fusion.4
  63.7 11.9 %fusion.18 = f32[30,20]{0,1:T(8,128)S(1)} fusion(f32[4,256,256]{2,0,1:T(4,128)S(1)} %broadcast_multiply_fusion.4, f32[20]{0:T(128)S(1)} %iota_add_fusion.4, f32[4,256,256]{2,0,1:T(4,128)S(1)} %copy.44, f32[30]{0:T(128)S(1)} %iota_add_fusion.5, f32[4,256,256]{2,0,1:T(4,128)S(1)} %copy.45, f32[30,20]{0,1:T(8,128)S(1)} %get-tuple-element.192, ...), kind=kOutput, calls=%fused_computation.19.clone.1 | convolution fusion | flops 385352896 | bytes 3150729 | tf_op jit(solution)/shard_map/while/body/eval_jaxpr/gkab,gjab->kj/dot_general | solution.py:38
  75.7 1.4 %fusion.17 = (f32[4,256,256]{2,1,0:T(8,128)S(1)}, f32[4,256,256]{2,1,0:T(8,128)S(1)}, f32[4,256,256]{2,1,0:T(8,128)S(1)}) fusion(f32[3]{0:T(128)S(1)} %get-tuple-element.207, f32[4,3,256]{2,1,0:T(4,128)S(1)} %get-tuple-element.175, f32[4,3,256]{2,1,0:T(4,128)S(1)} %get-tuple-element.176), kind=kLoop, calls=%fused_computation.15.clone.1 | loop fusion | flops 7077888 | bytes 3170316 | tf_op jit(solution)/shard_map/while/body/eval_jaxpr/reduce_sum | solution.py:25
  77.1 0.5 sqrt_multiply_fusion.2
  77.6 0.7 copy.44
  78.3 0.7 copy.45
  79.0 0.1 copy.43
  79.2 0.3 broadcast_multiply_fusion.4
  79.5 11.9 %fusion.18 = f32[30,20]{0,1:T(8,128)S(1)} fusion(f32[4,256,256]{2,0,1:T(4,128)S(1)} %broadcast_multiply_fusion.4, f32[20]{0:T(128)S(1)} %iota_add_fusion.4, f32[4,256,256]{2,0,1:T(4,128)S(1)} %copy.44, f32[30]{0:T(128)S(1)} %iota_add_fusion.5, f32[4,256,256]{2,0,1:T(4,128)S(1)} %copy.45, f32[30,20]{0,1:T(8,128)S(1)} %get-tuple-element.192, ...), kind=kOutput, calls=%fused_computation.19.clone.1 | convolution fusion | flops 385352896 | bytes 3150729 | tf_op jit(solution)/shard_map/while/body/eval_jaxpr/gkab,gjab->kj/dot_general | solution.py:38
  91.5 22.3 %psum.14 = f32[30,20]{0,1:T(8,128)S(1)} all-reduce(f32[30,20]{0,1:T(8,128)S(1)} %get-tuple-element.39), channel_id=1, replica_groups=mesh['gx'=4,'wa'=8] {'wa'}, use_global_device_ids=true, to_apply=%region_5.6 | all-reduce | flops 600 | bytes 4800 | tf_op jit(solution)/shard_map/psum | solution.py:79
  113.8 17.1 %psum.15 = f32[30,20]{0,1:T(8,128)S(1)} all-reduce(f32[30,20]{0,1:T(8,128)S(1)} %broadcast_multiply_fusion.2), channel_id=1, replica_groups=mesh['gx'=4,'wa'=8] {'gx'}, use_global_device_ids=true, to_apply=%region_6.7 | all-reduce | flops 600 | bytes 4800 | tf_op jit(solution)/shard_map/psum | solution.py:80
  130.9 0.6 broadcast_in_dim.24
  131.6 0.6 broadcast_multiply_fusion.1
  (40 shorter events, 0.6 us)
Async XLA Ops:
  0.6 8.8 %copy-start = (f32[16,3,256]{2,0,1:T(8,128)S(1)}, f32[16,3,256]{2,0,1:T(8,128)}, u32[]{:S(2)}) copy-start(f32[16,3,256]{2,0,1:T(8,128)} %param.9) | copy-start | bytes 147460
  0.6 27.5 %copy-start.1 = (f32[3]{0:T(128)S(1)}, f32[3]{0:T(128)}, u32[]{:S(2)}) copy-start(f32[3]{0:T(128)} %constant.46.clone..sunk.3) | copy-start | bytes 40
  3.5 10.0 %all-to-all-start.1 = ((f32[8,2,256]{2,1,0:T(2,128)}), f32[8,2,256]{2,1,0:T(2,128)S(1)}, u32[]{:S(2)}, u32[]{:S(2)}) async-start(f32[8,2,256]{2,1,0:T(2,128)} %reshape.132), calls=%async_computation.1 | async-start | bytes 32768 | tf_op jit(solution)/shard_map/all_to_all | solution.py:53
  13.5 8.2 %all-to-all-start = ((f32[8,2,3,256]{3,1,2,0:T(2,128)}), f32[8,2,3,256]{3,1,2,0:T(2,128)S(1)}, u32[]{:S(2)}, u32[]{:S(2)}) async-start(f32[8,2,3,256]{3,1,2,0:T(2,128)} %copy.31), calls=%async_computation | async-start | bytes 98304 | tf_op jit(solution)/shard_map/all_to_all | solution.py:52
  16.8 6.5 %collective-permute-start.1 = (f32[8,2,256]{2,1,0:T(2,128)S(1)}, f32[8,2,256]{2,1,0:T(2,128)S(1)}, u32[]{:S(2)}, u32[]{:S(2)}) collective-permute-start(f32[8,2,256]{2,1,0:T(2,128)S(1)} %all-to-all-done.1), channel_id=1, source_target_pairs={{0,8},{8,16},{16,24},{24,0},{1,9},{9,17},{17,25},{25,1},{2,10},{10... | collective-permute-start | bytes 49160 | tf_op jit(solution)/shard_map/ppermute | solution.py:15
  21.7 5.9 %collective-permute-start = (f32[8,2,3,256]{3,1,2,0:T(2,128)S(1)}, f32[8,2,3,256]{3,1,2,0:T(2,128)S(1)}, u32[]{:S(2)}, u32[]{:S(2)}) collective-permute-start(f32[8,2,3,256]{3,1,2,0:T(2,128)S(1)} %all-to-all-done), channel_id=1, source_target_pairs={{0,8},{8,16},{16,24},{24,0},{1,9},{9,17},{17,25},{25,1},{2,10},{10... | collective-permute-start | bytes 147464 | tf_op jit(solution)/shard_map/ppermute | solution.py:15
where the time goes:
time: 133 us; the launch traced here: 132 us
  matrix products  47.8 us (36%)
  blocking collectives  39.5 us (30%)
  starting transfers between devices  11.7 us (9%)
  local copies, waits for them, and re-layouts  11.3 us (8%)
  other arithmetic  11.2 us (8%)
  waiting for transfers between devices  8.92 us (7%)
  between operations  1.38 us (1%)
    dot_general x4, matrix products, group_counts(): jnp.einsum('gkab,gjab->kj', s_hat, m_hat, preferred_element_type=jnp.floa...  47.8 us
    psum x1, blocking collectives, per_device(): slab = lax.psum(total, 'wa') * scale  22.3 us
    psum x1, blocking collectives, per_device(): whole = lax.psum(slab, 'gx') / lax.axis_size('gx')  17.1 us
    reduce_sum x4, other arithmetic, group_counts(): jnp.sum(diff * middle, axis=1)  5.74 us
    all_to_all x1, starting transfers between devices, per_device(): lax.all_to_all(send_wgt, 'wa', split_axis=0, concat_axis=0, tiled=True)  5.2 us
    ppermute x2, waiting for transfers between devices, passed_along(): lax.ppermute(shard, axis, [(i, (i + by) % count) for i in range(count)])  3.6 us
    all_to_all x1, starting transfers between devices, per_device(): lax.all_to_all(send_pos, 'wa', split_axis=0, concat_axis=0, tiled=True)  3.35 us
    ppermute x2, starting transfers between devices, passed_along(): lax.ppermute(shard, axis, [(i, (i + by) % count) for i in range(count)])  3.21 us
  transfers between devices with their start and end apart: 4, of which 3 were waited for; matrix products, arithmetic and copies ran while one was open for 2% of the time, Pallas kernels for 0%

commit v1 on v0

--- a/solution.py
+++ b/solution.py
@@ -8,6 +8,11 @@
 reach = 0.5
 viewer = (0.5, 0.5, -1.5)
 units_per_turn = 4
+
+
+def gather_and_add(x, mesh_axis):
+    pieces = lax.all_gather(x, mesh_axis)
+    return jnp.sum(pieces, axis=0)
 
 
 def passed_along(shard, axis, by):
@@ -77,7 +82,7 @@
     total, _ = lax.scan(accumulate, start, items)
     scale = 10.0 * SBINS * MUBINS / (peers * units * block * block)
     slab = lax.psum(total, "wa") * scale
-    whole = lax.psum(slab, "gx") / lax.axis_size("gx")
+    whole = gather_and_add(slab, "gx") / lax.axis_size("gx")
     return (slab[None], whole)
 
 

time: 133 us -> 129 us (0.970)
  blocking collectives: 39.5 us -> 35.4 us
    psum x1 -> x0, blocking collectives: 17.1 us -> none  [per_device(): whole = lax.psum(slab, 'gx') / lax.axis_size('gx')]
    all_gather x0 -> x1, blocking collectives: none -> 13.1 us  [gather_and_add(): pieces = lax.all_gather(x, mesh_axis)]
where the time goes in v1:
time: 129 us; the launch traced here: 128 us
  matrix products  47.8 us (37%)
  blocking collectives  35.4 us (27%)
  starting transfers between devices  11.7 us (9%)
  local copies, waits for them, and re-layouts  11.3 us (9%)
  other arithmetic  11.2 us (9%)
  waiting for transfers between devices  8.92 us (7%)
  between operations  1.39 us (1%)
    dot_general x4, matrix products, group_counts(): jnp.einsum('gkab,gjab->kj', s_hat, m_hat, preferred_element_type=jnp.floa...  47.8 us
    psum x1, blocking collectives, per_device(): slab = lax.psum(total, 'wa') * scale  22.3 us
    all_gather x1, blocking collectives, gather_and_add(): pieces = lax.all_gather(x, mesh_axis)  13.1 us
    reduce_sum x4, other arithmetic, group_counts(): jnp.sum(diff * middle, axis=1)  5.74 us
    all_to_all x1, starting transfers between devices, per_device(): lax.all_to_all(send_wgt, 'wa', split_axis=0, concat_axis=0, tiled=True)  5.2 us
    ppermute x2, waiting for transfers between devices, passed_along(): lax.ppermute(shard, axis, [(i, (i + by) % count) for i in range(count)])  3.6 us
    all_to_all x1, starting transfers between devices, per_device(): lax.all_to_all(send_pos, 'wa', split_axis=0, concat_axis=0, tiled=True)  3.35 us
    ppermute x2, starting transfers between devices, passed_along(): lax.ppermute(shard, axis, [(i, (i + by) % count) for i in range(count)])  3.21 us
  transfers between devices with their start and end apart: 4, of which 3 were waited for; matrix products, arithmetic and copies ran while one was open for 2% of the time, Pallas kernels for 0%

profile of v1, /device:TPU:0, one launch (start us, length us, event | category | flops | bytes accessed | tf_op | source)
XLA Modules:
  0.0 128.1 jit_solution(15230465148569313329)
XLA Ops:
  0.7 0.8 copy.32
  1.5 0.8 fusion.12
  2.3 0.6 gather_fusion.2
  2.9 0.6 reshape.132
  3.5 5.2 %all-to-all-start.1 = ((f32[8,2,256]{2,1,0:T(2,128)}), f32[8,2,256]{2,1,0:T(2,128)S(1)}, u32[]{:S(2)}, u32[]{:S(2)}) async-start(f32[8,2,256]{2,1,0:T(2,128)} %reshape.132), calls=%async_computation.1 | async-start | bytes 32768 | tf_op jit(solution)/shard_map/all_to_all | solution.py:58
  8.7 0.7 fusion.14
  9.4 0.6 gather_fusion
  10.0 0.6 copy.33
  11.3 2.1 %all-to-all-done.1 = f32[8,2,256]{2,1,0:T(2,128)S(1)} async-done(((f32[8,2,256]{2,1,0:T(2,128)}), f32[8,2,256]{2,1,0:T(2,128)S(1)}, u32[]{:S(2)}, u32[]{:S(2)}) %all-to-all-start.1) | async-done | bytes 16416 | tf_op jit(solution)/shard_map/all_to_all | solution.py:58
  13.5 3.3 %all-to-all-start = ((f32[8,2,3,256]{3,1,2,0:T(2,128)}), f32[8,2,3,256]{3,1,2,0:T(2,128)S(1)}, u32[]{:S(2)}, u32[]{:S(2)}) async-start(f32[8,2,3,256]{3,1,2,0:T(2,128)} %copy.33), calls=%async_computation | async-start | bytes 98304 | tf_op jit(solution)/shard_map/all_to_all | solution.py:57
  16.8 1.6 %collective-permute-start.1 = (f32[8,2,256]{2,1,0:T(2,128)S(1)}, f32[8,2,256]{2,1,0:T(2,128)S(1)}, u32[]{:S(2)}, u32[]{:S(2)}) collective-permute-start(f32[8,2,256]{2,1,0:T(2,128)S(1)} %all-to-all-done.1), channel_id=1, source_target_pairs={{0,8},{8,16},{16,24},{24,0},{1,9},{9,17},{17,25},{25,1},{2,10},{10... | collective-permute-start | bytes 49160 | tf_op jit(solution)/shard_map/ppermute | solution.py:20
  18.5 3.2 %all-to-all-done = f32[8,2,3,256]{3,1,2,0:T(2,128)S(1)} async-done(((f32[8,2,3,256]{3,1,2,0:T(2,128)}), f32[8,2,3,256]{3,1,2,0:T(2,128)S(1)}, u32[]{:S(2)}, u32[]{:S(2)}) %all-to-all-start) | async-done | bytes 49184 | tf_op jit(solution)/shard_map/all_to_all | solution.py:57
  21.7 1.6 %collective-permute-start = (f32[8,2,3,256]{3,1,2,0:T(2,128)S(1)}, f32[8,2,3,256]{3,1,2,0:T(2,128)S(1)}, u32[]{:S(2)}, u32[]{:S(2)}) collective-permute-start(f32[8,2,3,256]{3,1,2,0:T(2,128)S(1)} %all-to-all-done), channel_id=1, source_target_pairs={{0,8},{8,16},{16,24},{24,0},{1,9},{9,17},{17,25},{25,1},{2,10},{10... | collective-permute-start | bytes 147464 | tf_op jit(solution)/shard_map/ppermute | solution.py:20
  23.4 0.6 gather_fusion.3
  24.0 3.6 %collective-permute-done = f32[8,2,3,256]{3,1,2,0:T(2,128)S(1)} collective-permute-done((f32[8,2,3,256]{3,1,2,0:T(2,128)S(1)}, f32[8,2,3,256]{3,1,2,0:T(2,128)S(1)}, u32[]{:S(2)}, u32[]{:S(2)}) %collective-permute-start) | collective-permute-done | bytes 49184 | tf_op jit(solution)/shard_map/ppermute | solution.py:20
  27.6 0.6 gather_fusion.1
  28.2 63.3 %while.12 = (s32[]{:T(128)}, f32[30,20]{0,1:T(8,128)S(1)}, f32[4,4,3,256]{3,2,1,0:T(4,128)S(1)}, f32[4,4,3,256]{3,2,1,0:T(4,128)S(1)}, f32[4,4,256]{2,1,0:T(4,12...) while((s32[]{:T(128)}, f32[30,20]{0,1:T(8,128)S(1)}, ...), condition=%wide.region_4.5_spmd.clone.clone, body=%wide.region_0.4_spmd.sunk.clone.clone.sunk | while | flops 394265856 | bytes 16889040 | solution.py:82
  28.2 1.4 %fusion.17 = (f32[4,256,256]{2,1,0:T(8,128)S(1)}, f32[4,256,256]{2,1,0:T(8,128)S(1)}, f32[4,256,256]{2,1,0:T(8,128)S(1)}) fusion(f32[3]{0:T(128)S(1)} %get-tuple-element.213, f32[4,3,256]{2,1,0:T(4,128)S(1)} %get-tuple-element.181, f32[4,3,256]{2,1,0:T(4,128)S(1)} %get-tuple-element.182), kind=kLoop, calls=%fused_computation.15.clone.1 | loop fusion | flops 7077888 | bytes 3170316 | tf_op jit(solution)/shard_map/while/body/eval_jaxpr/reduce_sum | solution.py:30
  29.7 0.5 sqrt_multiply_fusion.2
  30.2 0.7 copy.47
  30.8 0.7 copy.48
  31.5 0.1 copy.46
  31.7 0.3 broadcast_multiply_fusion.3
  32.1 11.9 %fusion.18 = f32[30,20]{0,1:T(8,128)S(1)} fusion(f32[4,256,256]{2,0,1:T(4,128)S(1)} %broadcast_multiply_fusion.3, f32[20]{0:T(128)S(1)} %iota_add_fusion.4, f32[4,256,256]{2,0,1:T(4,128)S(1)} %copy.47, f32[30]{0:T(128)S(1)} %iota_add_fusion.5, f32[4,256,256]{2,0,1:T(4,128)S(1)} %copy.48, f32[30,20]{0,1:T(8,128)S(1)} %get-tuple-element.198, ...), kind=kOutput, calls=%fused_computation.19.clone.1 | convolution fusion | flops 385352896 | bytes 3150729 | tf_op jit(solution)/shard_map/while/body/eval_jaxpr/gkab,gjab->kj/dot_general | solution.py:43
  44.1 1.4 %fusion.17 = (f32[4,256,256]{2,1,0:T(8,128)S(1)}, f32[4,256,256]{2,1,0:T(8,128)S(1)}, f32[4,256,256]{2,1,0:T(8,128)S(1)}) fusion(f32[3]{0:T(128)S(1)} %get-tuple-element.213, f32[4,3,256]{2,1,0:T(4,128)S(1)} %get-tuple-element.181, f32[4,3,256]{2,1,0:T(4,128)S(1)} %get-tuple-element.182), kind=kLoop, calls=%fused_computation.15.clone.1 | loop fusion | flops 7077888 | bytes 3170316 | tf_op jit(solution)/shard_map/while/body/eval_jaxpr/reduce_sum | solution.py:30
  45.5 0.5 sqrt_multiply_fusion.2
  46.0 0.7 copy.47
  46.7 0.7 copy.48
  47.4 0.1 copy.46
  47.5 0.3 broadcast_multiply_fusion.3
  47.9 11.9 %fusion.18 = f32[30,20]{0,1:T(8,128)S(1)} fusion(f32[4,256,256]{2,0,1:T(4,128)S(1)} %broadcast_multiply_fusion.3, f32[20]{0:T(128)S(1)} %iota_add_fusion.4, f32[4,256,256]{2,0,1:T(4,128)S(1)} %copy.47, f32[30]{0:T(128)S(1)} %iota_add_fusion.5, f32[4,256,256]{2,0,1:T(4,128)S(1)} %copy.48, f32[30,20]{0,1:T(8,128)S(1)} %get-tuple-element.198, ...), kind=kOutput, calls=%fused_computation.19.clone.1 | convolution fusion | flops 385352896 | bytes 3150729 | tf_op jit(solution)/shard_map/while/body/eval_jaxpr/gkab,gjab->kj/dot_general | solution.py:43
  59.9 1.4 %fusion.17 = (f32[4,256,256]{2,1,0:T(8,128)S(1)}, f32[4,256,256]{2,1,0:T(8,128)S(1)}, f32[4,256,256]{2,1,0:T(8,128)S(1)}) fusion(f32[3]{0:T(128)S(1)} %get-tuple-element.213, f32[4,3,256]{2,1,0:T(4,128)S(1)} %get-tuple-element.181, f32[4,3,256]{2,1,0:T(4,128)S(1)} %get-tuple-element.182), kind=kLoop, calls=%fused_computation.15.clone.1 | loop fusion | flops 7077888 | bytes 3170316 | tf_op jit(solution)/shard_map/while/body/eval_jaxpr/reduce_sum | solution.py:30
  61.3 0.5 sqrt_multiply_fusion.2
  61.8 0.7 copy.47
  62.5 0.7 copy.48
  63.3 0.3 broadcast_multiply_fusion.3
  63.7 11.9 %fusion.18 = f32[30,20]{0,1:T(8,128)S(1)} fusion(f32[4,256,256]{2,0,1:T(4,128)S(1)} %broadcast_multiply_fusion.3, f32[20]{0:T(128)S(1)} %iota_add_fusion.4, f32[4,256,256]{2,0,1:T(4,128)S(1)} %copy.47, f32[30]{0:T(128)S(1)} %iota_add_fusion.5, f32[4,256,256]{2,0,1:T(4,128)S(1)} %copy.48, f32[30,20]{0,1:T(8,128)S(1)} %get-tuple-element.198, ...), kind=kOutput, calls=%fused_computation.19.clone.1 | convolution fusion | flops 385352896 | bytes 3150729 | tf_op jit(solution)/shard_map/while/body/eval_jaxpr/gkab,gjab->kj/dot_general | solution.py:43
  75.7 1.4 %fusion.17 = (f32[4,256,256]{2,1,0:T(8,128)S(1)}, f32[4,256,256]{2,1,0:T(8,128)S(1)}, f32[4,256,256]{2,1,0:T(8,128)S(1)}) fusion(f32[3]{0:T(128)S(1)} %get-tuple-element.213, f32[4,3,256]{2,1,0:T(4,128)S(1)} %get-tuple-element.181, f32[4,3,256]{2,1,0:T(4,128)S(1)} %get-tuple-element.182), kind=kLoop, calls=%fused_computation.15.clone.1 | loop fusion | flops 7077888 | bytes 3170316 | tf_op jit(solution)/shard_map/while/body/eval_jaxpr/reduce_sum | solution.py:30
  77.1 0.5 sqrt_multiply_fusion.2
  77.6 0.7 copy.47
  78.3 0.7 copy.48
  79.0 0.1 copy.46
  79.2 0.3 broadcast_multiply_fusion.3
  79.5 11.9 %fusion.18 = f32[30,20]{0,1:T(8,128)S(1)} fusion(f32[4,256,256]{2,0,1:T(4,128)S(1)} %broadcast_multiply_fusion.3, f32[20]{0:T(128)S(1)} %iota_add_fusion.4, f32[4,256,256]{2,0,1:T(4,128)S(1)} %copy.47, f32[30]{0:T(128)S(1)} %iota_add_fusion.5, f32[4,256,256]{2,0,1:T(4,128)S(1)} %copy.48, f32[30,20]{0,1:T(8,128)S(1)} %get-tuple-element.198, ...), kind=kOutput, calls=%fused_computation.19.clone.1 | convolution fusion | flops 385352896 | bytes 3150729 | tf_op jit(solution)/shard_map/while/body/eval_jaxpr/gkab,gjab->kj/dot_general | solution.py:43
  91.5 22.3 %psum.7 = f32[30,20]{0,1:T(8,128)S(1)} all-reduce(f32[30,20]{0,1:T(8,128)S(1)} %get-tuple-element.39), channel_id=1, replica_groups=mesh['gx'=4,'wa'=8] {'wa'}, use_global_device_ids=true, to_apply=%region_5.6 | all-reduce | flops 600 | bytes 4800 | tf_op jit(solution)/shard_map/psum | solution.py:84
  113.8 13.1 %all-gather.1 = f32[4,30,20]{1,2,0:T(8,128)S(1)} all-gather(f32[1,30,20]{1,2,0:T(8,128)S(1)} %multiply_bitcast_fusion), channel_id=2, replica_groups=mesh['gx'=4,'wa'=8] {'gx'}, dimensions={0}, use_global_device_ids=true | all-gather | bytes 12000 | tf_op jit(solution)/shard_map/all_gather | solution.py:14
  126.9 0.6 copy.38
  127.5 0.6 broadcast_multiply_fusion.1
  (41 shorter events, 0.7 us)
Async XLA Ops:
  0.6 8.8 %copy-start = (f32[16,3,256]{2,0,1:T(8,128)S(1)}, f32[16,3,256]{2,0,1:T(8,128)}, u32[]{:S(2)}) copy-start(f32[16,3,256]{2,0,1:T(8,128)} %param.9) | copy-start | bytes 147460
  0.6 27.5 %copy-start.1 = (f32[3]{0:T(128)S(1)}, f32[3]{0:T(128)}, u32[]{:S(2)}) copy-start(f32[3]{0:T(128)} %constant.46.clone..sunk.3) | copy-start | bytes 40
  3.5 10.0 %all-to-all-start.1 = ((f32[8,2,256]{2,1,0:T(2,128)}), f32[8,2,256]{2,1,0:T(2,128)S(1)}, u32[]{:S(2)}, u32[]{:S(2)}) async-start(f32[8,2,256]{2,1,0:T(2,128)} %reshape.132), calls=%async_computation.1 | async-start | bytes 32768 | tf_op jit(solution)/shard_map/all_to_all | solution.py:58
  13.5 8.2 %all-to-all-start = ((f32[8,2,3,256]{3,1,2,0:T(2,128)}), f32[8,2,3,256]{3,1,2,0:T(2,128)S(1)}, u32[]{:S(2)}, u32[]{:S(2)}) async-start(f32[8,2,3,256]{3,1,2,0:T(2,128)} %copy.33), calls=%async_computation | async-start | bytes 98304 | tf_op jit(solution)/shard_map/all_to_all | solution.py:57
  16.8 6.5 %collective-permute-start.1 = (f32[8,2,256]{2,1,0:T(2,128)S(1)}, f32[8,2,256]{2,1,0:T(2,128)S(1)}, u32[]{:S(2)}, u32[]{:S(2)}) collective-permute-start(f32[8,2,256]{2,1,0:T(2,128)S(1)} %all-to-all-done.1), channel_id=1, source_target_pairs={{0,8},{8,16},{16,24},{24,0},{1,9},{9,17},{17,25},{25,1},{2,10},{10... | collective-permute-start | bytes 49160 | tf_op jit(solution)/shard_map/ppermute | solution.py:20
  21.7 5.9 %collective-permute-start = (f32[8,2,3,256]{3,1,2,0:T(2,128)S(1)}, f32[8,2,3,256]{3,1,2,0:T(2,128)S(1)}, u32[]{:S(2)}, u32[]{:S(2)}) collective-permute-start(f32[8,2,3,256]{3,1,2,0:T(2,128)S(1)} %all-to-all-done), channel_id=1, source_target_pairs={{0,8},{8,16},{16,24},{24,0},{1,9},{9,17},{17,25},{25,1},{2,10},{10... | collective-permute-start | bytes 147464 | tf_op jit(solution)/shard_map/ppermute | solution.py:20
